TPU v7x, 32 devices: a whole 2x2x4 slice. The times are simulated.
32 devices in a mesh: freq: 4 (over x, core), gblk: 8 (over z, y).
Axes of the slice: x: 2, y: 2, z: 4, core: 2. Of those that a mesh axis runs over, the one named last changes fastest.
Arguments:
- w_imag: bfloat16 [8, 8192, 16384], P('freq', 'gblk'), may hold values from -0.046875 to 0.046875
- w_real: bfloat16 [4, 8192, 16384], P('freq', 'gblk'), may hold values from -0.046875 to 0.046875
- pair_elements: bfloat16 [8192, 256], P('gblk'), may hold values from -0.75 to 0.75
- quad_weight: float32 [8, 128], P('freq'), may hold values from 0.1 to 1
- residue_freq: int32 [128], replicated, may hold values from 0 to 3
- owner_bands: int32 [128], replicated, may hold values from 0 to 127, each once
Outputs:
- sigma: float32 [128, 256], P(('freq', 'gblk'))
Inputs may be any that keep to these rules, and one draw needn't show every extreme that they name: `owner_bands`: each band appears once.
All inputs are finite; a program needn't handle non-finite values.
Results may differ from a plain program's by a relative error of at most 0.0003.
Values may be sent and summed in bfloat16 or wider, within the bound.
A program may use at most 192 MiB of HBM per device.

v0:
```python
import jax
import jax.numpy as jnp
from jax import lax
from jax.sharding import PartitionSpec as P


def on_device(w_imag, w_real, pair_elements, quad_weight, residue_freq, owner_bands):
    bands = pair_elements.shape[1] // 2
    g_count = w_imag.shape[2] // 2
    fr_local = w_real.shape[0]
    wide_elems = pair_elements.astype(jnp.float32)
    freq_first_index = lax.axis_index("freq") * fr_local
    real_ids = freq_first_index + jnp.arange(fr_local, dtype=jnp.int32)
    residue_weight = (residue_freq[None, :] == real_ids[:, None]).astype(jnp.float32)
    shard_rows = lax.all_gather(pair_elements, "gblk", axis=0, tiled=True)
    row_span = shard_rows.shape[0]
    lower_rows = jnp.concatenate([-shard_rows[:, bands:], shard_rows[:, :bands]], axis=1)

    def contrib(matrix):
        upper_cols = lax.slice_in_dim(matrix, 0, row_span, axis=2)
        lower_cols = lax.dynamic_slice_in_dim(matrix, g_count, row_span, 2)
        result = jnp.einsum(
            "frg,gc->frc", upper_cols, shard_rows, preferred_element_type=jnp.float32
        )
        return result + jnp.einsum(
            "frg,gc->frc", lower_cols, lower_rows, preferred_element_type=jnp.float32
        )

    x_imag = contrib(w_imag)
    x_real = contrib(w_real)

    def sandwich(products):
        blocks = jnp.einsum("gb,fgc->fbc", wide_elems, products, precision=lax.Precision.HIGHEST)
        sig_re = blocks[:, :bands, :bands] + blocks[:, bands:, bands:]
        sig_im = blocks[:, :bands, bands:] - blocks[:, bands:, :bands]
        return jnp.concatenate([sig_re, sig_im], axis=2)

    partial_value = jnp.sum(quad_weight[:, :, None] * sandwich(x_imag), axis=0)
    partial_value = partial_value + jnp.sum(residue_weight[:, :, None] * sandwich(x_real), axis=0)
    onehot = (owner_bands[:, None] == jnp.arange(bands, dtype=jnp.int32)[None, :]).astype(
        jnp.float32
    )
    permuted = jnp.dot(onehot, partial_value, precision=lax.Precision.HIGHEST)
    grouped = lax.psum_scatter(permuted, "freq", scatter_dimension=0, tiled=True)
    sigma = lax.psum_scatter(grouped, "gblk", scatter_dimension=0, tiled=True)
    return sigma


def solution(mesh):
    placed = (
        P("freq", "gblk", None),
        P("freq", "gblk", None),
        P("gblk", None),
        P("freq", None),
        P(),
        P(),
    )
    return jax.shard_map(
        on_device, mesh=mesh, in_specs=placed, out_specs=P(("freq", "gblk"), None), check_vma=False
    )
```

profile of v0, /device:TPU:0, one launch (start us, length us, event | category | flops | bytes accessed | tf_op | source)
XLA Modules:
  0.0 208.3 jit_solution(6413655461911375520)
XLA Ops:
  6.5 0.7 all-gather.2.cloned.1.call-update
  7.3 0.0 reduce-scatter.2.cloned.1.call-start
  7.3 0.7 compare_convert_fusion
  8.0 77.0 %all-gather.2.cloned.1.call-done = bf16[8192,256]{1,0:T(8,128)(2,1)} async-done(((bf16[1024,256]{1,0:T(8,128)(2,1)}), bf16[8192,256]{1,0:T(8,128)(2,1)}) %all-gather.2.cloned.1.call-update) | async-done | bytes 4194320 | tf_op jit(solution)/shard_map/all_gather | solution.py:15
  85.0 2.8 %slice_negate_fusion = (bf16[8192,128]{1,0:T(8,128)(2,1)S(1)}, bf16[8192,128]{1,0:T(8,128)(2,1)S(1)}) fusion(bf16[8192,256]{1,0:T(8,128)(2,1)} %all-gather.2.cloned.1.call-done), kind=kLoop, calls=%fused_computation.13 | loop fusion | flops 1048576 | bytes 8388608 | tf_op jit(solution)/shard_map/neg | solution.py:17
  87.8 0.7 copy-done.1
  88.5 9.6 %fusion.6 = f32[1024,256]{1,0:T(8,128)S(1)} fusion(bf16[8192,256]{1,0:T(8,128)(2,1)S(1)} %copy-done.1, bf16[1,1024,16384]{2,1,0:T(8,128)(2,1)} %param.7), kind=kOutput, calls=%fused_computation.6 | convolution fusion | flops 4294967296 | bytes 22020096 | tf_op jit(solution)/shard_map/frg,gc->frc/dot_general | solution.py:22
  98.1 0.0 copy-done.2
  98.1 0.0 copy-done.3
  98.1 11.3 %fusion.16 = f32[1024,256]{1,0:T(8,128)} fusion(f32[1024,256]{1,0:T(8,128)S(1)} %fusion.6, bf16[8192,128]{1,0:T(8,128)(2,1)S(1)} %get-tuple-element.6, bf16[8192,128]{1,0:T(8,128)(2,1)S(1)} %get-tuple-element.5, bf16[1,1024,16384]{2,1,0:T(8,128)(2,1)} %param.7), kind=kOutput, calls=%fused_computation.17 | convolution fusion | flops 4303618048 | bytes 23068672 | tf_op jit(solution)/shard_map/frg,gc->frc/dot_general | solution.py:25
  109.4 15.4 %fusion = f32[256,2,1024]{2,0,1:T(8,128)S(1)} fusion(bf16[2,1024,16384]{2,1,0:T(8,128)(2,1)} %param.6, bf16[8192,128]{1,0:T(8,128)(2,1)} %copy-done.3, bf16[8192,128]{1,0:T(8,128)(2,1)} %copy-done.2), kind=kOutput, calls=%fused_computation | convolution fusion | flops 8598323200 | bytes 39845888 | tf_op jit(solution)/shard_map/frg,gc->frc/dot_general | solution.py:25
  124.9 0.0 copy-done
  124.9 2.2 %convolution_bitcast_fusion = f32[1,256,256]{1,2,0:T(8,128)S(1)} fusion(f32[1024,256]{1,0:T(8,128)} %fusion.16, bf16[1024,256]{1,0:T(8,128)(2,1)S(1)} %copy-done), kind=kOutput, calls=%fused_computation.19 | convolution fusion | flops 805306368 | bytes 1835008 | tf_op jit(solution)/shard_map/gb,fgc->fbc/dot_general | solution.py:33
  127.1 15.4 %fusion.2 = f32[2,1024,256]{1,2,0:T(8,128)S(1)} fusion(bf16[2,1024,16384]{2,1,0:T(8,128)(2,1)} %param.6, bf16[8192,256]{1,0:T(8,128)(2,1)} %all-gather.2.cloned.1.call-done), kind=kOutput, calls=%fused_computation.2 | convolution fusion | flops 8589934592 | bytes 39845888 | tf_op jit(solution)/shard_map/frg,gc->frc/dot_general | solution.py:22
  142.5 0.0 copy-start.4
  142.5 0.0 copy-start.5
  142.6 0.0 copy-start.6
  142.6 1.2 fusion.19
  143.9 0.9 fusion.23
  144.8 0.0 reduce-scatter.2.cloned.1.call-update
  144.8 0.6 dynamic-slice
  146.1 17.1 %reduce-scatter.2.cloned.1.call-done = f32[32,256]{1,0:T(8,128)} async-done(((f32[128,256]{1,0:T(8,128)}), f32[32,256]{1,0:T(8,128)}) %reduce-scatter.2.cloned.1.call-update) | async-done | bytes 32784 | tf_op jit(solution)/shard_map/reduce_scatter | solution.py:44
  163.1 37.8 %all-reduce = f32[32,256]{1,0:T(8,128)S(1)} all-reduce(f32[32,256]{1,0:T(8,128)} %reduce-scatter.2.cloned.1.call-done), channel_id=3, replica_groups=mesh['freq'=4,'gblk'=8] {'gblk'}, use_global_device_ids=true, to_apply=%region_2.0.clone | all-reduce | flops 8192 | bytes 65536
  200.9 0.6 constant_dynamic-slice_fusion
  (11 shorter events, 0.1 us)
Async XLA Ops:
  6.5 78.5 %all-gather.2.cloned.1.call-start = ((), (), s32[]{:S(2)}) async-start(), calls=%async_computation.1 | async-start | bytes 4718592 | tf_op jit(solution)/shard_map/all_gather | solution.py:15
  7.3 155.9 %reduce-scatter.2.cloned.1.call-start = ((), (), s32[]{:S(2)}) async-start(), calls=%async_computation.2 | async-start | bytes 163840 | tf_op jit(solution)/shard_map/reduce_scatter | solution.py:44
  85.0 3.4 %copy-start.1 = (bf16[8192,256]{1,0:T(8,128)(2,1)S(1)}, bf16[8192,256]{1,0:T(8,128)(2,1)}, u32[]{:S(2)}) copy-start(bf16[8192,256]{1,0:T(8,128)(2,1)} %all-gather.2.cloned.1.call-done) | copy-start | bytes 12582916
  88.5 9.6 %copy-start.2 = (bf16[8192,128]{1,0:T(8,128)(2,1)}, bf16[8192,128]{1,0:T(8,128)(2,1)S(1)}, u32[]{:S(2)}) copy-start(bf16[8192,128]{1,0:T(8,128)(2,1)S(1)} %get-tuple-element.5) | copy-start | bytes 6291460
  88.5 9.7 %copy-start.3 = (bf16[8192,128]{1,0:T(8,128)(2,1)}, bf16[8192,128]{1,0:T(8,128)(2,1)S(1)}, u32[]{:S(2)}) copy-start(bf16[8192,128]{1,0:T(8,128)(2,1)S(1)} %get-tuple-element.6) | copy-start | bytes 6291460
  109.4 15.5 %copy-start = (bf16[1024,256]{1,0:T(8,128)(2,1)S(1)}, bf16[1024,256]{1,0:T(8,128)(2,1)}, u32[]{:S(2)}) copy-start(bf16[1024,256]{1,0:T(8,128)(2,1)} %param.8) | copy-start | bytes 1572868
  142.5 1.3 copy-start.4
  142.5 1.3 copy-start.5
  142.6 2.3 %copy-start.6 = (u32[32]{0:T(128)S(1)}, u32[32]{0:T(128)}, u32[]{:S(2)}) copy-start(u32[32]{0:T(128)} %constant.12) | copy-start | bytes 388
Sparse Core Ops, SparseCore 0:
  9.5 75.5 all-gather.1
  144.9 18.1 reduce-scatter.1
where the time goes:
time: 209 us; the launch traced here: 208 us
  waiting for transfers between devices  94.8 us (45%)
  matrix products  56.1 us (27%)
  blocking collectives  37.8 us (18%)
  between operations  14.2 us (7%)
  other arithmetic  3.5 us (2%)
    all_gather x1, waiting for transfers between devices, on_device(): shard_rows = lax.all_gather(pair_elements, 'gblk', axis=0, tiled=True)  77 us
    unnamed x1, blocking collectives  37.8 us
    dot_general x2, matrix products, contrib(): jnp.einsum('frg,gc->frc', lower_cols, lower_rows, preferred_element_type=...  26.8 us
    dot_general x2, matrix products, contrib(): jnp.einsum('frg,gc->frc', upper_cols, shard_rows, preferred_element_type=...  25 us
    reduce_scatter x1, waiting for transfers between devices, on_device(): lax.psum_scatter(permuted, 'freq', scatter_dimension=0, tiled=True)  17.1 us
  transfers between devices with their start and end apart: 2, of which 2 were waited for; matrix products, arithmetic and copies ran while one was open for 1% of the time, Pallas kernels for 0%

commit v1 on v0

v1 whole, which is shorter than its diff:
```python
import functools
import math

import jax
import jax.numpy as jnp
from jax import lax
from jax.experimental import pallas as pl
from jax.experimental.pallas import tpu as pltpu
from jax.sharding import PartitionSpec as P

MESH = pl.DeviceIdType.MESH
LANES = 256
BUFFERS = 3


def ring_position(index, n):
    z = index // 2
    return z + (index % 2) * (n - 1 - 2 * z)


def ring_index(position, n):
    low = (position < n // 2).astype(jnp.int32)
    return low * (2 * position) + (1 - low) * (2 * (n - 1 - position) + 1)


def self_energy_kernel(
    n, nf, pieces_half, tile,
    wi_hbm, wr_hbm, m_hbm, quad_ref, residue_ref, owner_ref, out_ref,
    wbuf, gath, left, weights, ubuf, acc, stage, inbox,
    w_sem, own_sem, ring_send, ring_recv, pair_send, pair_recv, out_send, out_recv,
):
    f = lax.axis_index("freq")
    me = lax.axis_index("gblk")
    pos = ring_position(me, n)
    core = f % 2
    fi, rows, width = wi_hbm.shape
    fr = wr_hbm.shape[0]
    g_count = width // 2
    bands = owner_ref.shape[1]
    piece_rows = gath.shape[2]
    per_block = rows // tile
    steps = n * per_block
    lag = min(2 * per_block, steps - 1)
    devices = n * nf
    mine = f * n + me

    def slot_of(k):
        d = (k + 1) // 2
        sign = 2 * (k % 2) - 1
        return lax.rem(pos - sign * d + 2 * n, n)

    def w_copies(t, slot):
        block = ring_index(slot_of(t // per_block), n)
        col = block * rows + (t % per_block) * tile
        copies = []
        for half in range(2):
            cols = pl.ds(pl.multiple_of(col + half * g_count, tile), tile)
            copies.append(pltpu.make_async_copy(
                wi_hbm.at[:, :, cols], wbuf.at[slot, half, pl.ds(0, fi)], w_sem.at[slot, half, 0]))
            copies.append(pltpu.make_async_copy(
                wr_hbm.at[:, :, cols], wbuf.at[slot, half, pl.ds(fi, fr)], w_sem.at[slot, half, 1]))
        return copies

    barrier = pltpu.get_barrier_semaphore()

    def greet(r, carry):
        other = lax.rem(mine + r, devices)
        pl.semaphore_signal(barrier, inc=1, device_id=(other // n, other % n), device_id_type=MESH)
        return carry

    lax.fori_loop(1, devices, greet, 0)

    own = [pltpu.make_async_copy(
        m_hbm.at[pl.ds(i * piece_rows, piece_rows)], gath.at[pos, i], own_sem.at[i])
        for i in range(2 * pieces_half)]
    for c in own:
        c.start()
    for t in range(min(BUFFERS - 1, steps)):
        for c in w_copies(t, t):
            c.start()

    onehot_t = (lax.broadcasted_iota(jnp.int32, (bands, bands), 0) == owner_ref[...]).astype(jnp.float32)
    onehot = jnp.transpose(onehot_t)
    first = f * fr
    for j in range(fi):
        weights[j] = jnp.sum(onehot * quad_ref[pl.ds(j, 1), :], axis=1, keepdims=True)
    for j in range(fr):
        row = (residue_ref[...] == first + j).astype(jnp.float32)
        weights[fi + j] = jnp.sum(onehot * row, axis=1, keepdims=True)
    acc[...] = jnp.zeros_like(acc)
    for c in own:
        c.wait()
    own_m = gath[pos].reshape(rows, 2 * bands)
    picker = onehot.astype(jnp.bfloat16)
    for half in range(2):
        left[pl.ds(half * bands, bands), :] = lax.dot_general(
            picker, own_m[:, half * bands:(half + 1) * bands], (((1,), (1,)), ((), ())),
            preferred_element_type=jnp.float32).astype(jnp.bfloat16)

    split = (pieces_half + 1) // 2

    def direction(k, q):
        if k == n - 1:
            return 1 if q < split or n == 2 else -1
        return 1 if k % 2 else -1

    def ring_copy(k, q, sending_slot, sign):
        to = ring_index(lax.rem(pos + sign + n, n), n)
        at = gath.at[sending_slot, core * pieces_half + q]
        return pltpu.make_async_remote_copy(
            src_ref=at, dst_ref=at, send_sem=ring_send.at[k, q], recv_sem=ring_recv.at[k, q],
            device_id=(f, to), device_id_type=MESH)

    def pair_copy(k, q, whose):
        at = gath.at[slot_of(k), whose * pieces_half + q]
        return pltpu.make_async_remote_copy(
            src_ref=at, dst_ref=at, send_sem=pair_send.at[k, q], recv_sem=pair_recv.at[k, q],
            device_id=(f + 1 - 2 * core, me), device_id_type=MESH)

    def outgoing():
        found = []
        for q in range(pieces_half):
            for k in range(1, n):
                sign = direction(k, q)
                if k <= 2 and (k < n - 1 or n == 2):
                    source = 0
                elif k < n - 1:
                    source = k - 2
                else:
                    source = n - 3 if sign == 1 else n - 2
                found.append((k, q, source, sign))
        return found

    sends = outgoing()

    def start_own():
        for k, q, source, sign in sends:
            if source == 0:
                ring_copy(k, q, pos, sign).start()

    def event(k, q):
        ring_copy(k, q, slot_of(k), direction(k, q)).wait_recv()
        for k2, q2, source, sign in sends:
            if source == k and q2 == q:
                ring_copy(k2, q, slot_of(k), sign).start()
        pair_copy(k, q, core).start()

    per_dir = max(1, (n // 2) * pieces_half - pieces_half // 2)
    events = {}
    for k in range(1, n):
        for q in range(pieces_half):
            if k == n - 1 and direction(k, q) == -1:
                m = (n // 2 - 1) * pieces_half + q - split
            else:
                m = ((k + 1) // 2 - 1) * pieces_half + q
            at = math.ceil(0.18 * steps + 0.65 * steps * (m + 1) / per_dir)
            at = max(1, min(at, steps - 1, lag + k * per_block))
            events.setdefault(at, []).append((m, k, q))

    def v_product(v):
        block = v // per_block
        count = tile // piece_rows
        rhs = gath[slot_of(block), pl.ds((v % per_block) * count, count)].reshape(tile, 2 * bands)
        return jnp.dot(ubuf[v], rhs, preferred_element_type=jnp.float32)

    def await_pair(k):
        for q in range(pieces_half):
            pair_copy(k, q, 1 - core).wait_recv()

    def step(t, with_v):
        slot = lax.rem(t, BUFFERS)
        ahead = t + BUFFERS - 1

        @pl.when(ahead < steps)
        def _():
            for c in w_copies(ahead, lax.rem(ahead, BUFFERS)):
                c.start()

        for at, group in sorted(events.items()):
            if (at >= lag) == with_v:
                @pl.when(t == at)
                def _(group=group):
                    for _m, k, q in sorted(group):
                        event(k, q)
        if with_v:
            for k in range(1, n):
                if lag + k * per_block < steps:
                    @pl.when(t == lag + k * per_block)
                    def _(k=k):
                        await_pair(k)
        for c in w_copies(t, slot):
            c.wait()
        if with_v:
            acc[...] += v_product(t - lag)
        lhs = left[...]
        ur = ui = None
        for j in range(fi + fr):
            tr = jnp.dot(lhs, wbuf[slot, 0, j], preferred_element_type=jnp.float32)
            ti = jnp.dot(lhs, wbuf[slot, 1, j], preferred_element_type=jnp.float32)
            w = weights[j]
            a = w * (tr[:bands] + ti[bands:])
            b = w * (ti[:bands] - tr[bands:])
            ur = a if ur is None else ur + a
            ui = b if ui is None else ui + b
        for i, value in enumerate((ur, ui)):
            high = value.astype(jnp.bfloat16)
            low = (value - high.astype(jnp.float32)).astype(jnp.bfloat16)
            ubuf[t, pl.ds(2 * i * bands, bands), :] = high
            ubuf[t, pl.ds((2 * i + 1) * bands, bands), :] = low

    step(0, False)
    pl.semaphore_wait(barrier, devices - 1)
    start_own()

    def early(t, carry):
        step(t, False)
        return carry

    def late(t, carry):
        step(t, True)
        return carry

    lax.fori_loop(1, lag, early, 0)
    lax.fori_loop(lag, steps, late, 0)

    for k in range(1, n):
        if lag + k * per_block >= steps:
            await_pair(k)
    total = acc[...]
    for v in range(steps - lag, steps):
        total = total + v_product(v)
    p = total[:bands] + total[bands:2 * bands]
    q = total[2 * bands:3 * bands] + total[3 * bands:]
    real = p[:, :bands] - q[:, bands:]
    imag = p[:, bands:] + q[:, :bands]
    share = out_ref.shape[0]
    for d in range(devices):
        stage[d, :, pl.ds(0, bands)] = real[d * share:(d + 1) * share]
        stage[d, :, pl.ds(bands, bands)] = imag[d * share:(d + 1) * share]

    def give(r, carry):
        other = lax.rem(mine + r, devices)
        pltpu.make_async_remote_copy(
            src_ref=stage.at[other], dst_ref=inbox.at[r - 1], send_sem=out_send, recv_sem=out_recv,
            device_id=(other // n, other % n), device_id_type=MESH).start()
        return carry

    lax.fori_loop(1, devices, give, 0)
    for k, q_, source, sign in sends:
        ring_copy(k, q_, pos if source == 0 else slot_of(source), sign).wait_send()
    for k in range(1, n):
        for q_ in range(pieces_half):
            pair_copy(k, q_, core).wait_send()
    pltpu.make_async_copy(inbox, inbox, out_recv).wait()
    out_ref[...] = stage[mine] + jnp.sum(inbox[...], axis=0)
    pltpu.make_async_copy(inbox, inbox, out_send).wait()


def on_device(n, nf, w_imag, w_real, pair_elements, quad_weight, residue_freq, owner_bands):
    fi, rows, width = w_imag.shape
    fr = w_real.shape[0]
    bands = owner_bands.shape[0]
    tile = min(512, rows)
    pieces_half = 2 if rows >= 1024 else 1
    piece_rows = rows // (2 * pieces_half)
    steps = n * (rows // tile)
    devices = n * nf
    share = bands // devices
    dma = pltpu.SemaphoreType.DMA
    anyspace = pl.BlockSpec(memory_space=pl.ANY)
    vmem = pl.BlockSpec(memory_space=pltpu.VMEM)
    flops = 2 * (fi + fr) * rows * width * 2 * bands
    return pl.pallas_call(
        functools.partial(self_energy_kernel, n, nf, pieces_half, tile),
        out_shape=jax.ShapeDtypeStruct((share, 2 * bands), jnp.float32),
        in_specs=[anyspace, anyspace, anyspace, vmem, vmem, vmem],
        out_specs=vmem,
        scratch_shapes=[
            pltpu.VMEM((BUFFERS, 2, fi + fr, rows, tile), jnp.bfloat16),
            pltpu.VMEM((n, 2 * pieces_half, piece_rows, 2 * bands), jnp.bfloat16),
            pltpu.VMEM((2 * bands, rows), jnp.bfloat16),
            pltpu.VMEM((fi + fr, bands, 1), jnp.float32),
            pltpu.VMEM((steps, 4 * bands, tile), jnp.bfloat16),
            pltpu.VMEM((4 * bands, 2 * bands), jnp.float32),
            pltpu.VMEM((devices, share, 2 * bands), jnp.float32),
            pltpu.VMEM((devices - 1, share, 2 * bands), jnp.float32),
            dma((BUFFERS, 2, 2)),
            dma((2 * pieces_half,)),
            dma((n, pieces_half)),
            dma((n, pieces_half)),
            dma((n, pieces_half)),
            dma((n, pieces_half)),
            dma,
            dma,
        ],
        compiler_params=pltpu.CompilerParams(
            collective_id=0, has_side_effects=True, vmem_limit_bytes=60 * 1024 * 1024),
        cost_estimate=pl.CostEstimate(
            flops=flops, bytes_accessed=(fi + fr) * rows * width * 2, transcendentals=0),
    )(w_imag, w_real, pair_elements, quad_weight,
      residue_freq.reshape(1, bands), owner_bands.reshape(1, bands))


def solution(mesh):
    placed = (
        P("freq", "gblk", None),
        P("freq", "gblk", None),
        P("gblk", None),
        P("freq", None),
        P(),
        P(),
    )
    body = functools.partial(on_device, mesh.shape["gblk"], mesh.shape["freq"])
    return jax.shard_map(
        body, mesh=mesh, in_specs=placed, out_specs=P(("freq", "gblk"), None), check_vma=False
    )
```

time: 209 us -> 54 us (0.26)
  waiting for transfers between devices: 94.8 us -> 0 us
  matrix products: 56.1 us -> 0 us
  Pallas kernels: 0 us -> 52.5 us
  blocking collectives: 37.8 us -> 0 us
  between operations: 14.2 us -> 0.01 us
  other arithmetic: 3.5 us -> 0 us
    all_gather x1 -> x0, waiting for transfers between devices: 77 us -> none  [on_device(): shard_rows = lax.all_gather(pair_elements, 'gblk', axis=0, tiled=True)]
    dot_general x7 -> x0, matrix products: 56.1 us -> none  [the longest x2 26.8 us: contrib(): jnp.einsum('frg,gc->frc', lower_cols, lower_rows, preferred_element_type=...]
    pallas_call x0 -> x1, Pallas kernels: none -> 52.5 us  [on_device(): pl.pallas_call(functools.partial(self_energy_kernel, n, nf, pieces_half,...]
    unnamed x1 -> x0, blocking collectives: 37.8 us -> none
    reduce_scatter x1 -> x0, waiting for transfers between devices: 17.1 us -> none  [on_device(): lax.psum_scatter(permuted, 'freq', scatter_dimension=0, tiled=True)]
    neg x1 -> x0, other arithmetic: 2.78 us -> none  [on_device(): -shard_rows[:, bands:]]
  transfers between devices with their start and end apart: 2 -> 0, of which waited for: 2 -> 0; matrix products, arithmetic and copies ran while one was open for 1% -> 0% of each run, Pallas kernels for 0% -> 0%
where the time goes in v1:
time: 54 us; the launch traced here: 53.8 us
  Pallas kernels  52.5 us (97%)
  local copies, waits for them, and re-layouts  1.28 us (2%)
    pallas_call x1, Pallas kernels, on_device(): pl.pallas_call(functools.partial(self_energy_kernel, n, nf, pieces_half,...  52.5 us
    unnamed x1, local copies, waits for them, and re-layouts  1.28 us

profile of v1, /device:TPU:0, one launch (start us, length us, event | category | flops | bytes accessed | tf_op | source)
XLA Modules:
  0.0 53.8 jit_solution(5946776549877727046)
XLA Ops:
  0.0 52.5 %shard_map.64 = f32[4,256]{1,0:T(4,128)} custom-call(bf16[2,1024,16384]{2,1,0:T(8,128)(2,1)} %wi_hbm.1, bf16[1,1024,16384]{2,1,0:T(8,128)(2,1)} %wr_hbm.1, bf16[1024,256]{1,0:T(8,128)(2,1)} %m_hbm.1, f32[2,128]{1,0:T(2,128)} %quad_ref.1, s32[1,128]{1,0:T(1,128)} %bitcast.2, s32[1,128]{1,0:T(1,128)} %bitcast.3), custom_call_target="tpu_custom_call" | custom-call | flops 25769803776 | bytes 100663296 | tf_op jit(solution)/shard_map/pallas_call | solution.py:273
  52.5 1.3 %copy.8 = f32[4,256]{1,0:T(4,128)} copy(f32[4,256]{1,0:T(4,128)} %shard_map.64) | data formatting | bytes 8192
